TPU v7x, 32 devices: a whole 2x2x4 slice. The times are simulated.
32 devices in a mesh: shots: 1, gx: 32 (over z, y, x, core), gy: 1.
Axes of the slice: x: 2, y: 2, z: 4, core: 2. Of those that a mesh axis runs over, the one named last changes fastest.
Arguments:
- pressure: float32 [128, 256, 128], P(None, ('shots', 'gx'), 'gy'), may hold values from -6 to 6
- pressure_prior: float32 [128, 256, 128], P(None, ('shots', 'gx'), 'gy'), may hold values from -6 to 6
- courant_square: bfloat16 [128, 256, 128], P(None, 'gx', 'gy'), may hold values from 0.049804688 to 0.1796875
- wavelet: float32 [16], P('shots'), may hold values from -4 to 4
- delay_steps: int32 [256, 128], P(('shots', 'gx'), 'gy'), may hold values from 0 to 7
- source_depth: int32 [256, 128], P(('shots', 'gx'), 'gy'), may hold values from 4 to 31
- receiver_depth: int32 [256, 128], P(('shots', 'gx'), 'gy'), may hold values from 0 to 31
- receiver_field: float32 [128, 256, 128], P(None, ('shots', 'gx'), 'gy'), may hold values from -6 to 6
Outputs:
- pressure_final: float32 [128, 256, 128], P(None, ('shots', 'gx'), 'gy')
- image: float32 [128, 256, 128], P('gx', 'shots', 'gy')
All inputs are finite; a program needn't handle non-finite values.
Results may differ from a plain program's by a relative error of at most 0.00035.
Values sent between devices are 32-bit elements; how exact they have to be, the bound alone decides.
A program may use at most 64 MiB of HBM per device.

v0:
```python
import functools

import jax
import jax.numpy as jnp
from jax import lax
from jax.experimental import pallas as pl
from jax.experimental.pallas import tpu as pltpu
from jax.sharding import PartitionSpec as P

STEPS = 8
REACH = 4
CENTER = -205.0 / 72.0
COEFS = (1.6, -0.2, 8.0 / 315.0, -1.0 / 560.0)
CHUNKS = 2
GROUP = 8


def kernel(
    nx,
    ny,
    pressure,
    prior,
    courant,
    wavelet,
    delay,
    sdepth,
    rdepth,
    receiver,
    final,
    image,
    field,
    side,
    prior_v,
    courant_v,
    receiver_v,
    amp,
    product,
    slab,
    weights,
    wave_v,
    delay_v,
    sdepth_v,
    rdepth_v,
    local_sem,
    send_sem,
    recv_sem,
    side_send,
    side_recv,
    out_sem,
    img_send,
    img_recv,
    known,
):
    depth, width, length = pressure.shape
    rows = depth // CHUNKS
    slab_depth = depth // nx
    me = lax.axis_index("gx")
    mine = lax.axis_index("gy")

    local = [
        pltpu.make_async_copy(
            pressure, field.at[0, pl.ds(REACH, depth), pl.ds(REACH, width), :], local_sem.at[0]
        ),
        pltpu.make_async_copy(prior, prior_v, local_sem.at[1]),
        pltpu.make_async_copy(courant, courant_v, local_sem.at[2]),
        pltpu.make_async_copy(receiver, receiver_v, local_sem.at[3]),
        pltpu.make_async_copy(wavelet, wave_v, local_sem.at[4]),
        pltpu.make_async_copy(delay, delay_v, local_sem.at[5]),
        pltpu.make_async_copy(sdepth, sdepth_v, local_sem.at[6]),
        pltpu.make_async_copy(rdepth, rdepth_v, local_sem.at[7]),
    ]
    for copy in local:
        copy.start()

    barrier = pltpu.get_barrier_semaphore()
    beside = sorted({1, nx - 1} - {0}) if nx > 1 else []
    for j in beside:
        pl.semaphore_signal(
            barrier,
            inc=1,
            device_id={"gx": lax.rem(me + j, nx)},
            device_id_type=pl.DeviceIdType.MESH,
        )
    for j in range(1, ny):
        pl.semaphore_signal(
            barrier,
            inc=1,
            device_id={"gy": lax.rem(mine + j, ny)},
            device_id_type=pl.DeviceIdType.MESH,
        )

    rim = jnp.zeros((REACH, width + 2 * REACH, length), jnp.float32)
    for t in range(STEPS):
        field[t, pl.ds(0, REACH), :, :] = rim
        field[t, pl.ds(REACH + depth, REACH), :, :] = rim

    def clear(at):
        def one(i, carry):
            t = i // CHUNKS
            c = i % CHUNKS
            field[t, pl.ds(REACH + c * rows, rows), pl.ds(at, REACH), :] = jnp.zeros(
                (rows, REACH, length), jnp.float32
            )
            return carry

        lax.fori_loop(0, STEPS * CHUNKS, one, 0)

    @pl.when(me == 0)
    def _():
        clear(0)

    @pl.when(me == nx - 1)
    def _():
        clear(REACH + width)

    if ny > 1:

        def clear_side(k):
            def one(i, carry):
                t = i // CHUNKS
                c = i % CHUNKS
                side[t, k, pl.ds(c * rows, rows), :, :] = jnp.zeros(
                    (rows, width, length), jnp.float32
                )
                return carry

            lax.fori_loop(0, STEPS * CHUNKS, one, 0)

        @pl.when(mine == 0)
        def _():
            clear_side(0)

        @pl.when(mine == ny - 1)
        def _():
            clear_side(1)

    local[4].wait()
    local[5].wait()
    late = delay_v[...]
    for t in range(STEPS):
        total = jnp.zeros((width, length), jnp.float32)
        for pick in range(wavelet.shape[0]):
            total = total + jnp.where(late + t == pick, wave_v[pick], 0.0)
        amp[t] = total

    if len(beside) + ny > 1:
        pl.semaphore_wait(barrier, len(beside) + ny - 1)

    def span(c):
        return pl.ds(REACH + c * rows, rows)

    def face(t, c, way):
        source = REACH + width - REACH if way == 0 else REACH
        target = 0 if way == 0 else REACH + width
        peer = lax.rem(me + 1, nx) if way == 0 else lax.rem(me + nx - 1, nx)
        return pltpu.make_async_remote_copy(
            src_ref=field.at[t, span(c), pl.ds(source, REACH), :],
            dst_ref=field.at[t, span(c), pl.ds(target, REACH), :],
            send_sem=send_sem.at[t, c, way],
            recv_sem=recv_sem.at[t, c, way],
            device_id={"gx": peer},
            device_id_type=pl.DeviceIdType.MESH,
        )

    def flank(t, c, way):
        peer = lax.rem(mine + 1, ny) if way == 0 else lax.rem(mine + ny - 1, ny)
        return pltpu.make_async_remote_copy(
            src_ref=field.at[t, span(c), pl.ds(REACH, width), :],
            dst_ref=side.at[t, way, pl.ds(c * rows, rows), :, :],
            send_sem=side_send.at[t, c, way],
            recv_sem=side_recv.at[t, c, way],
            device_id={"gy": peer},
            device_id_type=pl.DeviceIdType.MESH,
        )

    def each_face(t, c, act, sending):
        lower, upper = (me > 0, me < nx - 1)
        if nx > 1:
            for way in (0, 1):
                there = upper if (way == 0) == sending else lower

                @pl.when(there)
                def _():
                    act(face(t, c, way))

        if ny > 1:
            for way in (0, 1):
                there = mine < ny - 1 if (way == 0) == sending else mine > 0

                @pl.when(there)
                def _():
                    act(flank(t, c, way))

    def send(t, c):
        each_face(t, c, lambda copy: copy.start(), True)

    def sent(t, c):
        each_face(t, c, lambda copy: copy.wait_send(), True)

    def arrived(t, c):
        each_face(t, c, lambda copy: copy.wait_recv(), False)

    local[0].wait()
    for c in range(CHUNKS):
        send(0, c)
    local[1].wait()
    local[2].wait()

    lanes = lax.broadcasted_iota(jnp.int32, (width, length), 1)
    start = lax.broadcasted_iota(jnp.int32, (length, length), 0)
    gap = jnp.abs(start - lax.broadcasted_iota(jnp.int32, (length, length), 1))
    band = jnp.where(gap == 0, 3.0 * CENTER, 0.0)
    for k in range(1, REACH + 1):
        band = jnp.where(gap == k, COEFS[k - 1], band)
    band_high = band.astype(jnp.bfloat16)
    band_low = (band - band_high.astype(jnp.float32)).astype(jnp.bfloat16)
    weights[...] = jnp.concatenate(
        [
            jnp.concatenate([band_high, band_low], axis=1),
            jnp.concatenate([band_high, jnp.zeros_like(band_low)], axis=1),
        ],
        axis=0,
    )

    def along(v):
        tall = v.reshape(GROUP * width, length)
        high = tall.astype(jnp.bfloat16)
        low = (tall - high.astype(jnp.float32)).astype(jnp.bfloat16)
        both = jnp.dot(
            jnp.concatenate([high, low], axis=1), weights[...], preferred_element_type=jnp.float32
        )
        return (both[:, :length] + both[:, length:]).reshape(GROUP, width, length)

    local[6].wait()
    origin = sdepth_v[...]

    def advance(t, z, old):
        own = pl.ds(REACH, width)
        v = field[t, pl.ds(REACH + z, GROUP), own, :]
        total = (3.0 * CENTER) * v if ny > 1 else along(v)
        for k in range(1, REACH + 1):
            near = (
                field[t, pl.ds(REACH + z + k, GROUP), own, :]
                + field[t, pl.ds(REACH + z - k, GROUP), own, :]
            )
            near = near + (
                field[t, pl.ds(REACH + z, GROUP), pl.ds(REACH + k, width), :]
                + field[t, pl.ds(REACH + z, GROUP), pl.ds(REACH - k, width), :]
            )
            total = total + COEFS[k - 1] * near
            if ny > 1:
                up = pltpu.roll(v, length - k, 2)
                down = pltpu.roll(v, k, 2)
                low = pltpu.roll(side[t, 0, pl.ds(z, GROUP), :, :], k, 2)
                high = pltpu.roll(side[t, 1, pl.ds(z, GROUP), :, :], length - k, 2)
                up = jnp.where((lanes < length - k)[None], up, high)
                down = jnp.where((lanes >= k)[None], down, low)
                total = total + COEFS[k - 1] * (up + down)
        strength = courant_v[pl.ds(z, GROUP), :, :].astype(jnp.float32)
        levels = lax.broadcasted_iota(jnp.int32, (GROUP, width, length), 0) + z
        shot = jnp.where(levels == origin[None], amp[t][None], 0.0)
        return 2.0 * v - old + strength * total + shot

    def first_chunk(c, carry):
        arrived(0, c)

        def group(g, inner):
            z = c * rows + g * GROUP
            new = advance(0, z, prior_v[pl.ds(z, GROUP), :, :])
            field[1, pl.ds(REACH + z, GROUP), pl.ds(REACH, width), :] = new
            return inner

        lax.fori_loop(0, rows // GROUP, group, 0, unroll=True)
        send(1, c)
        return carry

    lax.fori_loop(0, CHUNKS, first_chunk, 0)

    reach = []
    while (reach[-1] * 2 if reach else 1) < nx // 2:
        reach.append(reach[-1] * 2 if reach else 1)

    def greet(number):
        for way, j in enumerate((reach[number], nx - reach[number])):
            pl.semaphore_signal(
                known.at[number, way],
                inc=1,
                device_id={"gx": lax.rem(me + j, nx)},
                device_id_type=pl.DeviceIdType.MESH,
            )

    def greeted(number):
        for way in (0, 1):
            pl.semaphore_wait(known.at[number, way], 1)

    def meet(number):
        if number > 0:
            greeted(number - 1)
        greet(number)

    def step(i, carry):
        t = i // CHUNKS
        c = i % CHUNKS
        for number in range(len(reach)):
            if CHUNKS + 3 * number < STEPS * CHUNKS:

                @pl.when(i == CHUNKS + 3 * number)
                def _():
                    meet(number)

        arrived(t, c)

        def group(g, inner):
            z = c * rows + g * GROUP
            old = field[t - 1, pl.ds(REACH + z, GROUP), pl.ds(REACH, width), :]
            new = advance(t, z, old)
            field[t + 1, pl.ds(REACH + z, GROUP), pl.ds(REACH, width), :] = new
            return inner

        lax.fori_loop(0, rows // GROUP, group, 0, unroll=True)

        @pl.when(t < STEPS - 1)
        def _():
            send(t + 1, c)

        return carry

    lax.fori_loop(CHUNKS, STEPS * CHUNKS, step, 0)
    for number in range(len(reach)):
        if CHUNKS + 3 * number >= STEPS * CHUNKS:
            meet(number)
    if reach:
        greeted(len(reach) - 1)

    done = pltpu.make_async_copy(
        field.at[STEPS, pl.ds(REACH, depth), pl.ds(REACH, width), :], final, out_sem.at[0]
    )
    done.start()

    local[3].wait()
    local[7].wait()
    ground = rdepth_v[...]
    product[pl.ds(0, 1), :, :] = jnp.zeros((1, width, length), jnp.float32)
    product[pl.ds(depth + 1, 1), :, :] = jnp.zeros((1, width, length), jnp.float32)

    def multiply(g, carry):
        z = g * GROUP
        levels = lax.broadcasted_iota(jnp.int32, (GROUP, width, length), 0) + z
        masked = jnp.where(levels >= ground[None], receiver_v[pl.ds(z, GROUP), :, :], 0.0)
        product[pl.ds(1 + z, GROUP), :, :] = (
            field[STEPS, pl.ds(REACH + z, GROUP), pl.ds(REACH, width), :] * masked
        )
        return carry

    lax.fori_loop(0, depth // GROUP, multiply, 0)

    def landing(who):
        return image.at[:, pl.ds(pl.multiple_of(who * width, width), width), :]

    def piece(peer):
        return pltpu.make_async_remote_copy(
            src_ref=slab.at[pl.ds(peer * slab_depth, slab_depth), :, :],
            dst_ref=landing(me),
            send_sem=img_send.at[peer],
            recv_sem=img_recv.at[me],
            device_id={"gx": peer},
            device_id_type=pl.DeviceIdType.MESH,
        )

    def kept():
        return pltpu.make_async_copy(
            slab.at[pl.ds(me * slab_depth, slab_depth), :, :], landing(me), out_sem.at[1]
        )

    def filtered(peer):
        z = peer * slab_depth
        slab[pl.ds(z, slab_depth), :, :] = (
            2.0 * product[pl.ds(1 + z, slab_depth), :, :]
            - product[pl.ds(z, slab_depth), :, :]
            - product[pl.ds(2 + z, slab_depth), :, :]
        )

    def ship(j, carry):
        peer = lax.rem(me + j, nx)
        filtered(peer)
        piece(peer).start()
        return carry

    lax.fori_loop(1, nx, ship, 0)
    filtered(me)
    kept().start()

    def drain(i, carry):
        sent(i // CHUNKS, i % CHUNKS)
        return carry

    lax.fori_loop(0, STEPS * CHUNKS, drain, 0)

    def finish(j, carry):
        peer = lax.rem(me + j, nx)
        piece(peer).wait_send()
        came = lax.rem(me + nx - j, nx)
        pltpu.make_async_remote_copy(
            src_ref=slab.at[pl.ds(me * slab_depth, slab_depth), :, :],
            dst_ref=landing(came),
            send_sem=img_send.at[came],
            recv_sem=img_recv.at[came],
            device_id={"gx": came},
            device_id_type=pl.DeviceIdType.MESH,
        ).wait_recv()
        return carry

    lax.fori_loop(1, nx, finish, 0)
    kept().wait()
    done.wait()


def solution(mesh):
    nx, ny = mesh.shape["gx"], mesh.shape["gy"]

    def shards(
        pressure, prior, courant, wavelet, delay, sdepth, rdepth, receiver
    ):
        depth, width, length = pressure.shape
        hbm = pl.BlockSpec(memory_space=pl.ANY)
        flat = (depth, width, length)
        sides = (STEPS, 2, depth, width, length) if ny > 1 else (1, 1, 1, width, length)
        return pl.pallas_call(
            functools.partial(kernel, nx, ny),
            out_shape=(
                jax.ShapeDtypeStruct(flat, jnp.float32),
                jax.ShapeDtypeStruct((depth // nx, width * nx, length), jnp.float32),
            ),
            in_specs=[hbm] * 8,
            out_specs=(hbm, hbm),
            scratch_shapes=[
                pltpu.VMEM((STEPS + 1, depth + 2 * REACH, width + 2 * REACH, length), jnp.float32),
                pltpu.VMEM(sides, jnp.float32),
                pltpu.VMEM(flat, jnp.float32),
                pltpu.VMEM(flat, jnp.bfloat16),
                pltpu.VMEM(flat, jnp.float32),
                pltpu.VMEM((STEPS, width, length), jnp.float32),
                pltpu.VMEM((depth + 2, width, length), jnp.float32),
                pltpu.VMEM(flat, jnp.float32),
                pltpu.VMEM((2 * length, 2 * length), jnp.bfloat16),
                pltpu.SMEM(wavelet.shape, jnp.float32),
                pltpu.VMEM((width, length), jnp.int32),
                pltpu.VMEM((width, length), jnp.int32),
                pltpu.VMEM((width, length), jnp.int32),
                pltpu.SemaphoreType.DMA((8,)),
                pltpu.SemaphoreType.DMA((STEPS, CHUNKS, 2)),
                pltpu.SemaphoreType.DMA((STEPS, CHUNKS, 2)),
                pltpu.SemaphoreType.DMA((STEPS, CHUNKS, 2)),
                pltpu.SemaphoreType.DMA((STEPS, CHUNKS, 2)),
                pltpu.SemaphoreType.DMA((2,)),
                pltpu.SemaphoreType.DMA((nx,)),
                pltpu.SemaphoreType.DMA((nx,)),
                pltpu.SemaphoreType.REGULAR((max(nx.bit_length(), 1), 2)),
            ],
            compiler_params=pltpu.CompilerParams(
                collective_id=0, has_side_effects=True, vmem_limit_bytes=67043328
            ),
        )(pressure, prior, courant, wavelet, delay, sdepth, rdepth, receiver)

    in_specs = (
        P(None, ("shots", "gx"), "gy"),
        P(None, ("shots", "gx"), "gy"),
        P(None, "gx", "gy"),
        P("shots"),
        P(("shots", "gx"), "gy"),
        P(("shots", "gx"), "gy"),
        P(("shots", "gx"), "gy"),
        P(None, ("shots", "gx"), "gy"),
    )
    out_specs = (P(None, ("shots", "gx"), "gy"), P("gx", "shots", "gy"))
    return jax.shard_map(shards, mesh=mesh, in_specs=in_specs, out_specs=out_specs, check_vma=False)
```

profile of v0, /device:TPU:15, one launch (start us, length us, event | category | flops | bytes accessed | tf_op | source)
XLA Modules:
  0.0 69.2 jit_solution(1266980511837446637)
XLA Ops:
  0.6 65.9 %shard_map.95 = (f32[128,8,128]{2,1,0:T(8,128)}, f32[4,256,128]{2,1,0:T(8,128)}) custom-call(f32[128,8,128]{2,1,0:T(8,128)} %pressure.1, f32[128,8,128]{2,1,0:T(8,128)} %prior.1, bf16[128,8,128]{2,1,0:T(8,128)(2,1)} %courant.1, f32[16]{0:T(128)} %wavelet.1, s32[8,128]{1,0:T(8,128)} %delay.1, s32[8,128]{1,0:T(8,128)} %sdepth.1, s32[8,128]{1,0:T(8,128)} %rdepth.1, ...), custom_call_target="tpu_custom_call" | custom-call | tf_op jit(solution)/shard_map/pallas_call | solution.py:428
  66.5 0.0 copy-start
  66.5 1.9 %copy.12 = f32[128,8,128]{2,1,0:T(8,128)} copy(f32[128,8,128]{2,1,0:T(8,128)} %get-tuple-element.4) | data formatting | bytes 1048576
  68.5 0.0 copy-done
  68.5 0.8 %copy.13 = f32[4,256,128]{2,1,0:T(8,128)} copy(f32[4,256,128]{2,1,0:T(8,128)S(1)} %copy-done) | data formatting | bytes 1048576
Async XLA Ops:
  66.5 1.9 %copy-start = (f32[4,256,128]{2,1,0:T(8,128)S(1)}, f32[4,256,128]{2,1,0:T(8,128)}, u32[]{:S(2)}) copy-start(f32[4,256,128]{2,1,0:T(8,128)} %get-tuple-element.5) | copy-start | bytes 1572868
where the time goes:
time: 69.8 us; the launch traced here: 69.2 us
  Pallas kernels  65.9 us (94%)
  local copies, waits for them, and re-layouts  2.72 us (4%)
    pallas_call x1, Pallas kernels, shards(): pl.pallas_call(functools.partial(kernel, nx, ny), out_shape=(jax.ShapeDty...  65.9 us
    unnamed x4, local copies, waits for them, and re-layouts  2.72 us

commit v1 on v0

v1 whole, which is shorter than its diff:
```python
import functools

import jax
import jax.numpy as jnp
from jax import lax
from jax.experimental import pallas as pl
from jax.experimental.pallas import tpu as pltpu
from jax.sharding import PartitionSpec as P

STEPS = 8
REACH = 4
CENTER = -205.0 / 72.0
COEFS = (1.6, -0.2, 8.0 / 315.0, -1.0 / 560.0)
GROUP = 8


def chunks_of(depth):
    quarter = depth // 4
    return ((0, quarter), (depth - quarter, quarter), (quarter, depth - 2 * quarter))


def kernel(
    nx,
    ny,
    pressure,
    prior,
    courant,
    wavelet,
    delay,
    sdepth,
    rdepth,
    receiver,
    final,
    image,
    field,
    side,
    courant_v,
    receiver_v,
    amp,
    product,
    slab,
    weights,
    wave_v,
    delay_v,
    sdepth_v,
    rdepth_v,
    first_sem,
    local_sem,
    send_sem,
    recv_sem,
    side_send,
    side_recv,
    img_send,
    img_recv,
    known,
):
    depth, width, length = pressure.shape
    chunks = chunks_of(depth)
    slab_depth = depth // nx
    me = lax.axis_index("gx")
    mine = lax.axis_index("gy")
    own = pl.ds(REACH, width)

    barrier = pltpu.get_barrier_semaphore()

    def toward(way, far):
        return (me + far, me + far < nx) if way == 0 else (me - far, me >= far)

    if nx > 1:
        for way in (0, 1):
            peer, there = toward(way, 1)

            @pl.when(there)
            def _():
                pl.semaphore_signal(
                    barrier,
                    inc=1,
                    device_id={"gx": peer},
                    device_id_type=pl.DeviceIdType.MESH,
                )

    for j in range(1, ny):
        pl.semaphore_signal(
            barrier,
            inc=1,
            device_id={"gy": lax.rem(mine + j, ny)},
            device_id_type=pl.DeviceIdType.MESH,
        )

    first = [
        pltpu.make_async_copy(
            pressure.at[pl.ds(z, rows), :, :],
            field.at[1, pl.ds(REACH + z, rows), own, :],
            first_sem.at[c],
        )
        for c, (z, rows) in enumerate(chunks)
    ]
    local = [
        pltpu.make_async_copy(prior, field.at[0, pl.ds(REACH, depth), own, :], local_sem.at[0]),
        pltpu.make_async_copy(courant, courant_v, local_sem.at[1]),
        pltpu.make_async_copy(wavelet, wave_v, local_sem.at[2]),
        pltpu.make_async_copy(delay, delay_v, local_sem.at[3]),
        pltpu.make_async_copy(sdepth, sdepth_v, local_sem.at[4]),
        pltpu.make_async_copy(rdepth, rdepth_v, local_sem.at[5]),
        pltpu.make_async_copy(receiver, receiver_v, local_sem.at[6]),
    ]
    for copy in first + local:
        copy.start()

    def span(c):
        z, rows = chunks[c]
        return pl.ds(REACH + z, rows)

    def face(t, c, way):
        source = width if way == 0 else REACH
        target = 0 if way == 0 else REACH + width
        return pltpu.make_async_remote_copy(
            src_ref=field.at[t + 1, span(c), pl.ds(source, REACH), :],
            dst_ref=field.at[t + 1, span(c), pl.ds(target, REACH), :],
            send_sem=send_sem.at[t, c, way],
            recv_sem=recv_sem.at[t, c, way],
            device_id={"gx": lax.rem(me + (1 if way == 0 else nx - 1), nx)},
            device_id_type=pl.DeviceIdType.MESH,
        )

    def flank(t, c, way):
        peer = lax.rem(mine + 1, ny) if way == 0 else lax.rem(mine + ny - 1, ny)
        z, rows = chunks[c]
        return pltpu.make_async_remote_copy(
            src_ref=field.at[t + 1, span(c), own, :],
            dst_ref=side.at[t, way, pl.ds(z, rows), :, :],
            send_sem=side_send.at[t, c, way],
            recv_sem=side_recv.at[t, c, way],
            device_id={"gy": peer},
            device_id_type=pl.DeviceIdType.MESH,
        )

    def each_face(t, c, act, sending):
        if nx > 1:
            for way in (0, 1):
                there = me < nx - 1 if (way == 0) == sending else me > 0

                @pl.when(there)
                def _():
                    act(face(t, c, way))

        if ny > 1:
            for way in (0, 1):
                there = mine < ny - 1 if (way == 0) == sending else mine > 0

                @pl.when(there)
                def _():
                    act(flank(t, c, way))

    def send(t, c):
        each_face(t, c, lambda copy: copy.start(), True)

    def sent(t, c):
        each_face(t, c, lambda copy: copy.wait_send(), True)

    def arrived(t, c):
        each_face(t, c, lambda copy: copy.wait_recv(), False)

    beside = (me > 0).astype(jnp.int32) + (me < nx - 1).astype(jnp.int32)
    if nx > 1 or ny > 1:
        pl.semaphore_wait(barrier, beside + ny - 1)

    for c in range(len(chunks)):
        first[c].wait()
        send(0, c)

    rim = jnp.zeros((REACH, width + 2 * REACH, length), jnp.float32)
    for t in range(STEPS):
        field[t + 1, pl.ds(0, REACH), :, :] = rim
        field[t + 1, pl.ds(REACH + depth, REACH), :, :] = rim

    def clear(at):
        def one(t, carry):
            field[t + 1, pl.ds(REACH, depth), pl.ds(at, REACH), :] = jnp.zeros(
                (depth, REACH, length), jnp.float32
            )
            return carry

        lax.fori_loop(0, STEPS, one, 0)

    @pl.when(me == 0)
    def _():
        clear(0)

    @pl.when(me == nx - 1)
    def _():
        clear(REACH + width)

    if ny > 1:

        def clear_side(k):
            def one(t, carry):
                side[t, k] = jnp.zeros((depth, width, length), jnp.float32)
                return carry

            lax.fori_loop(0, STEPS, one, 0)

        @pl.when(mine == 0)
        def _():
            clear_side(0)

        @pl.when(mine == ny - 1)
        def _():
            clear_side(1)

    product[pl.ds(0, 1), :, :] = jnp.zeros((1, width, length), jnp.float32)
    product[pl.ds(depth + 1, 1), :, :] = jnp.zeros((1, width, length), jnp.float32)

    start = lax.broadcasted_iota(jnp.int32, (length, length), 0)
    gap = jnp.abs(start - lax.broadcasted_iota(jnp.int32, (length, length), 1))
    band = jnp.where(gap == 0, 3.0 * CENTER, 0.0)
    for k in range(1, REACH + 1):
        band = jnp.where(gap == k, COEFS[k - 1], band)
    band_high = band.astype(jnp.bfloat16)
    band_low = (band - band_high.astype(jnp.float32)).astype(jnp.bfloat16)
    weights[...] = jnp.concatenate(
        [
            jnp.concatenate([band_high, band_low], axis=1),
            jnp.concatenate([band_high, jnp.zeros_like(band_low)], axis=1),
        ],
        axis=0,
    )

    for copy in local[:6]:
        copy.wait()
    late = delay_v[...]
    for t in range(STEPS):
        total = jnp.zeros((width, length), jnp.float32)
        for pick in range(wavelet.shape[0]):
            total = total + jnp.where(late + t == pick, wave_v[pick], 0.0)
        amp[t] = total

    lanes = lax.broadcasted_iota(jnp.int32, (width, length), 1)
    origin = sdepth_v[...]

    def along(v):
        tall = v.reshape(GROUP * width, length)
        high = tall.astype(jnp.bfloat16)
        low = (tall - high.astype(jnp.float32)).astype(jnp.bfloat16)
        both = jnp.dot(
            jnp.concatenate([high, low], axis=1), weights[...], preferred_element_type=jnp.float32
        )
        return (both[:, :length] + both[:, length:]).reshape(GROUP, width, length)

    def advance(t, z):
        at = t + 1
        v = field[at, pl.ds(REACH + z, GROUP), own, :]
        old = field[t, pl.ds(REACH + z, GROUP), own, :]
        total = (3.0 * CENTER) * v if ny > 1 else along(v)
        for k in range(1, REACH + 1):
            near = (
                field[at, pl.ds(REACH + z + k, GROUP), own, :]
                + field[at, pl.ds(REACH + z - k, GROUP), own, :]
            )
            near = near + (
                field[at, pl.ds(REACH + z, GROUP), pl.ds(REACH + k, width), :]
                + field[at, pl.ds(REACH + z, GROUP), pl.ds(REACH - k, width), :]
            )
            total = total + COEFS[k - 1] * near
            if ny > 1:
                up = pltpu.roll(v, length - k, 2)
                down = pltpu.roll(v, k, 2)
                low = pltpu.roll(side[t, 0, pl.ds(z, GROUP), :, :], k, 2)
                high = pltpu.roll(side[t, 1, pl.ds(z, GROUP), :, :], length - k, 2)
                up = jnp.where((lanes < length - k)[None], up, high)
                down = jnp.where((lanes >= k)[None], down, low)
                total = total + COEFS[k - 1] * (up + down)
        strength = courant_v[pl.ds(z, GROUP), :, :].astype(jnp.float32)
        levels = lax.broadcasted_iota(jnp.int32, (GROUP, width, length), 0) + z
        shot = jnp.where(levels == origin[None], amp[t][None], 0.0)
        return 2.0 * v - old + strength * total + shot

    reach = []
    while (reach[-1] * 2 if reach else 1) < nx:
        reach.append(reach[-1] * 2 if reach else 1)

    def greet(number):
        for way in (0, 1):
            peer, there = toward(way, reach[number])

            @pl.when(there)
            def _():
                pl.semaphore_signal(
                    known.at[number, way],
                    inc=1,
                    device_id={"gx": peer},
                    device_id_type=pl.DeviceIdType.MESH,
                )

    def greeted(number):
        for way in (0, 1):
            there = toward(1 - way, reach[number])[1]

            @pl.when(there)
            def _():
                pl.semaphore_wait(known.at[number, way], 1)

    def meet(number):
        if number > 0:
            greeted(number - 1)
        greet(number)

    def step(t, carry):
        for number in range(len(reach)):
            if number + 1 < STEPS - 1:

                @pl.when(t == number + 1)
                def _():
                    meet(number)

        for c, (begin, rows) in enumerate(chunks):
            arrived(t, c)

            def group(g, inner):
                z = begin + g * GROUP
                field[t + 2, pl.ds(REACH + z, GROUP), own, :] = advance(t, z)
                return inner

            lax.fori_loop(0, rows // GROUP, group, 0, unroll=True)
            send(t + 1, c)
        return carry

    lax.fori_loop(0, STEPS - 1, step, 0)
    for number in range(len(reach)):
        if number + 1 >= STEPS - 1:
            meet(number)
    if reach:
        greeted(len(reach) - 1)

    def landing(who):
        return image.at[:, pl.ds(pl.multiple_of(who * width, width), width), :]

    def piece(peer):
        return pltpu.make_async_remote_copy(
            src_ref=slab.at[pl.ds(peer * slab_depth, slab_depth), :, :],
            dst_ref=landing(me),
            send_sem=img_send.at[peer],
            recv_sem=img_recv.at[me],
            device_id={"gx": peer},
            device_id_type=pl.DeviceIdType.MESH,
        )

    def filtered(peer):
        z = peer * slab_depth
        return (
            2.0 * product[pl.ds(1 + z, slab_depth), :, :]
            - product[pl.ds(z, slab_depth), :, :]
            - product[pl.ds(2 + z, slab_depth), :, :]
        )

    def ship(low, count):
        def one(j, carry):
            peer = low + lax.rem(me + 1 + j, count)
            value = filtered(peer)

            @pl.when(peer != me)
            def _():
                slab[pl.ds(peer * slab_depth, slab_depth), :, :] = value
                piece(peer).start()

            @pl.when(peer == me)
            def _():
                landing(me)[...] = value

            return carry

        lax.fori_loop(0, count, one, 0)

    local[6].wait()
    ground = rdepth_v[...]
    last = STEPS - 1
    ready, gone = set(), set()
    for c, (begin, rows) in enumerate(chunks):
        arrived(last, c)

        def group(g, inner):
            z = begin + g * GROUP
            new = advance(last, z)
            final[pl.ds(z, GROUP), :, :] = new
            levels = lax.broadcasted_iota(jnp.int32, (GROUP, width, length), 0) + z
            masked = jnp.where(levels >= ground[None], receiver_v[pl.ds(z, GROUP), :, :], 0.0)
            product[pl.ds(1 + z, GROUP), :, :] = new * masked
            return inner

        lax.fori_loop(0, rows // GROUP, group, 0, unroll=True)
        ready |= set(range(begin, begin + rows))
        able = [
            peer
            for peer in range(nx)
            if peer not in gone
            and all(
                level in ready
                for level in range(
                    max(peer * slab_depth - 1, 0), min((peer + 1) * slab_depth + 1, depth)
                )
            )
        ]
        gone |= set(able)
        low = 0
        while low < len(able):
            high = low + 1
            while high < len(able) and able[high] == able[high - 1] + 1:
                high += 1
            ship(able[low], high - low)
            low = high

    def drain(t, carry):
        for c in range(len(chunks)):
            sent(t, c)
        return carry

    lax.fori_loop(0, STEPS, drain, 0)

    def finish(j, carry):
        peer = lax.rem(me + j, nx)
        piece(peer).wait_send()
        came = lax.rem(me + nx - j, nx)
        pltpu.make_async_remote_copy(
            src_ref=slab.at[pl.ds(me * slab_depth, slab_depth), :, :],
            dst_ref=landing(came),
            send_sem=img_send.at[came],
            recv_sem=img_recv.at[came],
            device_id={"gx": came},
            device_id_type=pl.DeviceIdType.MESH,
        ).wait_recv()
        return carry

    lax.fori_loop(1, nx, finish, 0)


def solution(mesh):
    nx, ny = mesh.shape["gx"], mesh.shape["gy"]

    def shards(pressure, prior, courant, wavelet, delay, sdepth, rdepth, receiver):
        depth, width, length = pressure.shape
        parts = len(chunks_of(depth))
        hbm = pl.BlockSpec(memory_space=pl.ANY)
        vmem = pl.BlockSpec(memory_space=pltpu.VMEM)
        flat = (depth, width, length)
        sides = (STEPS, 2, depth, width, length) if ny > 1 else (1, 1, 1, width, length)
        return pl.pallas_call(
            functools.partial(kernel, nx, ny),
            out_shape=(
                pltpu.VMEM(flat, jnp.float32),
                pltpu.VMEM((depth // nx, width * nx, length), jnp.float32),
            ),
            in_specs=[hbm] * 8,
            out_specs=(vmem, vmem),
            scratch_shapes=[
                pltpu.VMEM((STEPS + 1, depth + 2 * REACH, width + 2 * REACH, length), jnp.float32),
                pltpu.VMEM(sides, jnp.float32),
                pltpu.VMEM(flat, jnp.bfloat16),
                pltpu.VMEM(flat, jnp.float32),
                pltpu.VMEM((STEPS, width, length), jnp.float32),
                pltpu.VMEM((depth + 2, width, length), jnp.float32),
                pltpu.VMEM(flat, jnp.float32),
                pltpu.VMEM((2 * length, 2 * length), jnp.bfloat16),
                pltpu.SMEM(wavelet.shape, jnp.float32),
                pltpu.VMEM((width, length), jnp.int32),
                pltpu.VMEM((width, length), jnp.int32),
                pltpu.VMEM((width, length), jnp.int32),
                pltpu.SemaphoreType.DMA((parts,)),
                pltpu.SemaphoreType.DMA((7,)),
                pltpu.SemaphoreType.DMA((STEPS, parts, 2)),
                pltpu.SemaphoreType.DMA((STEPS, parts, 2)),
                pltpu.SemaphoreType.DMA((STEPS, parts, 2)),
                pltpu.SemaphoreType.DMA((STEPS, parts, 2)),
                pltpu.SemaphoreType.DMA((nx,)),
                pltpu.SemaphoreType.DMA((nx,)),
                pltpu.SemaphoreType.REGULAR((max(nx.bit_length(), 1), 2)),
            ],
            compiler_params=pltpu.CompilerParams(
                collective_id=0, has_side_effects=True, vmem_limit_bytes=60000000
            ),
        )(pressure, prior, courant, wavelet, delay, sdepth, rdepth, receiver)

    in_specs = (
        P(None, ("shots", "gx"), "gy"),
        P(None, ("shots", "gx"), "gy"),
        P(None, "gx", "gy"),
        P("shots"),
        P(("shots", "gx"), "gy"),
        P(("shots", "gx"), "gy"),
        P(("shots", "gx"), "gy"),
        P(None, ("shots", "gx"), "gy"),
    )
    out_specs = (P(None, ("shots", "gx"), "gy"), P("gx", "shots", "gy"))
    return jax.shard_map(shards, mesh=mesh, in_specs=in_specs, out_specs=out_specs, check_vma=False)
```

time: 69.8 us -> 67.5 us (0.967); the launches traced: 69.2 us -> 66.1 us
  Pallas kernels: 65.9 us -> 63.9 us
  local copies, waits for them, and re-layouts: 2.72 us -> 1.59 us
    pallas_call x1, Pallas kernels: 65.9 us -> 63.9 us  [shards(): pl.pallas_call(functools.partial(kernel, nx, ny), out_shape=(pltpu.VMEM(f...]
    unnamed x4 -> x2, local copies, waits for them, and re-layouts: 2.72 us -> 1.59 us
where the time goes in v1:
time: 67.5 us; the launch traced here: 66.1 us
  Pallas kernels  63.9 us (95%)
  local copies, waits for them, and re-layouts  1.59 us (2%)
    pallas_call x1, Pallas kernels, shards(): pl.pallas_call(functools.partial(kernel, nx, ny), out_shape=(pltpu.VMEM(f...  63.9 us
    unnamed x2, local copies, waits for them, and re-layouts  1.59 us

profile of v1, /device:TPU:15, one launch (start us, length us, event | category | flops | bytes accessed | tf_op | source)
XLA Modules:
  0.0 66.1 jit_solution(4657375452652278646)
XLA Ops:
  0.6 63.9 %shard_map.95 = (f32[128,8,128]{2,1,0:T(8,128)S(1)}, f32[4,256,128]{2,1,0:T(8,128)S(1)}) custom-call(f32[128,8,128]{2,1,0:T(8,128)} %pressure.1, f32[128,8,128]{2,1,0:T(8,128)} %prior.1, bf16[128,8,128]{2,1,0:T(8,128)(2,1)} %courant.1, f32[16]{0:T(128)} %wavelet.1, s32[8,128]{1,0:T(8,128)} %delay.1, s32[8,128]{1,0:T(8,128)} %sdepth.1, s32[8,128]{1,0:T(8,128)} %rdepth.1, ...), custom_call_target="tpu_custom_call" | custom-call | tf_op jit(solution)/shard_map/pallas_call | solution.py:446
  64.5 0.8 %copy.12 = f32[128,8,128]{2,1,0:T(8,128)} copy(f32[128,8,128]{2,1,0:T(8,128)S(1)} %get-tuple-element.2) | data formatting | bytes 1048576
  65.3 0.8 %copy.13 = f32[4,256,128]{2,1,0:T(8,128)} copy(f32[4,256,128]{2,1,0:T(8,128)S(1)} %get-tuple-element.3) | data formatting | bytes 1048576

commit v2 on v1

--- a/solution.py
+++ b/solution.py
@@ -16,7 +16,7 @@
 
 def chunks_of(depth):
     quarter = depth // 4
-    return ((0, quarter), (depth - quarter, quarter), (quarter, depth - 2 * quarter))
+    return tuple((quarter * c, quarter) for c in (0, 3, 1, 2))
 
 
 def kernel(
@@ -104,45 +104,47 @@
         pltpu.make_async_copy(rdepth, rdepth_v, local_sem.at[5]),
         pltpu.make_async_copy(receiver, receiver_v, local_sem.at[6]),
     ]
-    for copy in first + local:
-        copy.start()
-
     def span(c):
         z, rows = chunks[c]
         return pl.ds(REACH + z, rows)
 
-    def face(t, c, way):
-        source = width if way == 0 else REACH
+    def face(t, c, way, opening):
+        z, rows = chunks[c]
+        source = width - REACH if way == 0 else 0
         target = 0 if way == 0 else REACH + width
         return pltpu.make_async_remote_copy(
-            src_ref=field.at[t + 1, span(c), pl.ds(source, REACH), :],
+            src_ref=pressure.at[pl.ds(z, rows), pl.ds(source, REACH), :]
+            if opening
+            else field.at[t + 1, span(c), pl.ds(REACH + source, REACH), :],
             dst_ref=field.at[t + 1, span(c), pl.ds(target, REACH), :],
-            send_sem=send_sem.at[t, c, way],
-            recv_sem=recv_sem.at[t, c, way],
+            send_sem=send_sem.at[t % 2, c, way],
+            recv_sem=recv_sem.at[t % 2, c, way],
             device_id={"gx": lax.rem(me + (1 if way == 0 else nx - 1), nx)},
             device_id_type=pl.DeviceIdType.MESH,
         )
 
-    def flank(t, c, way):
+    def flank(t, c, way, opening):
         peer = lax.rem(mine + 1, ny) if way == 0 else lax.rem(mine + ny - 1, ny)
         z, rows = chunks[c]
         return pltpu.make_async_remote_copy(
-            src_ref=field.at[t + 1, span(c), own, :],
+            src_ref=pressure.at[pl.ds(z, rows), :, :]
+            if opening
+            else field.at[t + 1, span(c), own, :],
             dst_ref=side.at[t, way, pl.ds(z, rows), :, :],
-            send_sem=side_send.at[t, c, way],
-            recv_sem=side_recv.at[t, c, way],
+            send_sem=side_send.at[t % 2, c, way],
+            recv_sem=side_recv.at[t % 2, c, way],
             device_id={"gy": peer},
             device_id_type=pl.DeviceIdType.MESH,
         )
 
-    def each_face(t, c, act, sending):
+    def each_face(t, c, act, sending, opening=False):
         if nx > 1:
             for way in (0, 1):
                 there = me < nx - 1 if (way == 0) == sending else me > 0
 
                 @pl.when(there)
                 def _():
-                    act(face(t, c, way))
+                    act(face(t, c, way, opening))
 
         if ny > 1:
             for way in (0, 1):
@@ -150,10 +152,10 @@
 
                 @pl.when(there)
                 def _():
-                    act(flank(t, c, way))
-
-    def send(t, c):
-        each_face(t, c, lambda copy: copy.start(), True)
+                    act(flank(t, c, way, opening))
+
+    def send(t, c, opening=False):
+        each_face(t, c, lambda copy: copy.start(), True, opening)
 
     def sent(t, c):
         each_face(t, c, lambda copy: copy.wait_send(), True)
@@ -166,8 +168,9 @@
         pl.semaphore_wait(barrier, beside + ny - 1)
 
     for c in range(len(chunks)):
-        first[c].wait()
-        send(0, c)
+        send(0, c, opening=True)
+    for copy in first + local:
+        copy.start()
 
     rim = jnp.zeros((REACH, width + 2 * REACH, length), jnp.float32)
     for t in range(STEPS):
@@ -226,7 +229,7 @@
         axis=0,
     )
 
-    for copy in local[:6]:
+    for copy in first + local[:6]:
         copy.wait()
     late = delay_v[...]
     for t in range(STEPS):
@@ -322,6 +325,11 @@
                 return inner
 
             lax.fori_loop(0, rows // GROUP, group, 0, unroll=True)
+
+            @pl.when(t > 0)
+            def _():
+                sent(t - 1, c)
+
             send(t + 1, c)
         return carry
 
@@ -339,8 +347,8 @@
         return pltpu.make_async_remote_copy(
             src_ref=slab.at[pl.ds(peer * slab_depth, slab_depth), :, :],
             dst_ref=landing(me),
-            send_sem=img_send.at[peer],
-            recv_sem=img_recv.at[me],
+            send_sem=img_send,
+            recv_sem=img_recv,
             device_id={"gx": peer},
             device_id_type=pl.DeviceIdType.MESH,
         )
@@ -409,28 +417,20 @@
             ship(able[low], high - low)
             low = high
 
-    def drain(t, carry):
+    for t in range(max(STEPS - 2, 0), STEPS):
         for c in range(len(chunks)):
             sent(t, c)
-        return carry
-
-    lax.fori_loop(0, STEPS, drain, 0)
-
-    def finish(j, carry):
-        peer = lax.rem(me + j, nx)
-        piece(peer).wait_send()
-        came = lax.rem(me + nx - j, nx)
-        pltpu.make_async_remote_copy(
-            src_ref=slab.at[pl.ds(me * slab_depth, slab_depth), :, :],
-            dst_ref=landing(came),
-            send_sem=img_send.at[came],
-            recv_sem=img_recv.at[came],
-            device_id={"gx": came},
+    if nx > 1:
+        others = pltpu.make_async_remote_copy(
+            src_ref=slab.at[pl.ds(0, (nx - 1) * slab_depth), :, :],
+            dst_ref=image.at[:, pl.ds(0, (nx - 1) * width), :],
+            send_sem=img_send,
+            recv_sem=img_recv,
+            device_id={"gx": lax.rem(me + 1, nx)},
             device_id_type=pl.DeviceIdType.MESH,
-        ).wait_recv()
-        return carry
-
-    lax.fori_loop(1, nx, finish, 0)
+        )
+        others.wait_send()
+        others.wait_recv()
 
 
 def solution(mesh):
@@ -466,13 +466,13 @@
                 pltpu.VMEM((width, length), jnp.int32),
                 pltpu.SemaphoreType.DMA((parts,)),
                 pltpu.SemaphoreType.DMA((7,)),
-                pltpu.SemaphoreType.DMA((STEPS, parts, 2)),
-                pltpu.SemaphoreType.DMA((STEPS, parts, 2)),
-                pltpu.SemaphoreType.DMA((STEPS, parts, 2)),
-                pltpu.SemaphoreType.DMA((STEPS, parts, 2)),
-                pltpu.SemaphoreType.DMA((nx,)),
-                pltpu.SemaphoreType.DMA((nx,)),
-                pltpu.SemaphoreType.REGULAR((max(nx.bit_length(), 1), 2)),
+                pltpu.SemaphoreType.DMA((2, parts, 2)),
+                pltpu.SemaphoreType.DMA((2, parts, 2)),
+                pltpu.SemaphoreType.DMA((2, parts, 2) if ny > 1 else (1, 1, 1)),
+                pltpu.SemaphoreType.DMA((2, parts, 2) if ny > 1 else (1, 1, 1)),
+                pltpu.SemaphoreType.DMA,
+                pltpu.SemaphoreType.DMA,
+                pltpu.SemaphoreType.REGULAR((max((nx - 1).bit_length(), 1), 2)),
             ],
             compiler_params=pltpu.CompilerParams(
                 collective_id=0, has_side_effects=True, vmem_limit_bytes=60000000

time: 67.5 us -> 63.4 us (0.939); the launches traced: 66.1 us -> 63.3 us
  Pallas kernels: 63.9 us -> 61 us
    pallas_call x1, Pallas kernels: 63.9 us -> 61 us  [shards(): pl.pallas_call(functools.partial(kernel, nx, ny), out_shape=(pltpu.VMEM(f...]
where the time goes in v2:
time: 63.4 us; the launch traced here: 63.3 us
  Pallas kernels  61 us (96%)
  local copies, waits for them, and re-layouts  1.59 us (3%)
  between operations  0.64 us (1%)
    pallas_call x1, Pallas kernels, shards(): pl.pallas_call(functools.partial(kernel, nx, ny), out_shape=(pltpu.VMEM(f...  61 us
    unnamed x2, local copies, waits for them, and re-layouts  1.59 us

profile of v2, /device:TPU:15, one launch (start us, length us, event | category | flops | bytes accessed | tf_op | source)
XLA Modules:
  0.0 63.3 jit_solution(7439101784853410485)
XLA Ops:
  0.6 61.0 %shard_map.95 = (f32[128,8,128]{2,1,0:T(8,128)S(1)}, f32[4,256,128]{2,1,0:T(8,128)S(1)}) custom-call(f32[128,8,128]{2,1,0:T(8,128)} %pressure.1, f32[128,8,128]{2,1,0:T(8,128)} %prior.1, bf16[128,8,128]{2,1,0:T(8,128)(2,1)} %courant.1, f32[16]{0:T(128)} %wavelet.1, s32[8,128]{1,0:T(8,128)} %delay.1, s32[8,128]{1,0:T(8,128)} %sdepth.1, s32[8,128]{1,0:T(8,128)} %rdepth.1, ...), custom_call_target="tpu_custom_call" | custom-call | tf_op jit(solution)/shard_map/pallas_call | solution.py:446
  61.7 0.8 %copy.12 = f32[128,8,128]{2,1,0:T(8,128)} copy(f32[128,8,128]{2,1,0:T(8,128)S(1)} %get-tuple-element.2) | data formatting | bytes 1048576
  62.5 0.8 %copy.13 = f32[4,256,128]{2,1,0:T(8,128)} copy(f32[4,256,128]{2,1,0:T(8,128)S(1)} %get-tuple-element.3) | data formatting | bytes 1048576

commit v3 on v2

--- a/solution.py
+++ b/solution.py
@@ -44,7 +44,6 @@
     delay_v,
     sdepth_v,
     rdepth_v,
-    first_sem,
     local_sem,
     send_sem,
     recv_sem,
@@ -87,14 +86,6 @@
             device_id_type=pl.DeviceIdType.MESH,
         )
 
-    first = [
-        pltpu.make_async_copy(
-            pressure.at[pl.ds(z, rows), :, :],
-            field.at[1, pl.ds(REACH + z, rows), own, :],
-            first_sem.at[c],
-        )
-        for c, (z, rows) in enumerate(chunks)
-    ]
     local = [
         pltpu.make_async_copy(prior, field.at[0, pl.ds(REACH, depth), own, :], local_sem.at[0]),
         pltpu.make_async_copy(courant, courant_v, local_sem.at[1]),
@@ -103,6 +94,7 @@
         pltpu.make_async_copy(sdepth, sdepth_v, local_sem.at[4]),
         pltpu.make_async_copy(rdepth, rdepth_v, local_sem.at[5]),
         pltpu.make_async_copy(receiver, receiver_v, local_sem.at[6]),
+        pltpu.make_async_copy(pressure, field.at[1, pl.ds(REACH, depth), own, :], local_sem.at[7]),
     ]
     def span(c):
         z, rows = chunks[c]
@@ -169,7 +161,7 @@
 
     for c in range(len(chunks)):
         send(0, c, opening=True)
-    for copy in first + local:
+    for copy in local[::-1]:
         copy.start()
 
     rim = jnp.zeros((REACH, width + 2 * REACH, length), jnp.float32)
@@ -229,7 +221,7 @@
         axis=0,
     )
 
-    for copy in first + local[:6]:
+    for copy in local[:6] + local[7:]:
         copy.wait()
     late = delay_v[...]
     for t in range(STEPS):
@@ -319,17 +311,16 @@
         for c, (begin, rows) in enumerate(chunks):
             arrived(t, c)
 
+            @pl.when(t > 0)
+            def _():
+                sent(t - 1, c)
+
             def group(g, inner):
                 z = begin + g * GROUP
                 field[t + 2, pl.ds(REACH + z, GROUP), own, :] = advance(t, z)
                 return inner
 
             lax.fori_loop(0, rows // GROUP, group, 0, unroll=True)
-
-            @pl.when(t > 0)
-            def _():
-                sent(t - 1, c)
-
             send(t + 1, c)
         return carry
 
@@ -433,6 +424,17 @@
         others.wait_recv()
 
 
+def store(final_v, image_v, final, image, sem):
+    copies = (
+        pltpu.make_async_copy(final_v, final, sem.at[0]),
+        pltpu.make_async_copy(image_v, image, sem.at[1]),
+    )
+    for copy in copies:
+        copy.start()
+    for copy in copies:
+        copy.wait()
+
+
 def solution(mesh):
     nx, ny = mesh.shape["gx"], mesh.shape["gy"]
 
@@ -443,11 +445,12 @@
         vmem = pl.BlockSpec(memory_space=pltpu.VMEM)
         flat = (depth, width, length)
         sides = (STEPS, 2, depth, width, length) if ny > 1 else (1, 1, 1, width, length)
-        return pl.pallas_call(
+        deep = (depth // nx, width * nx, length)
+        held = pl.pallas_call(
             functools.partial(kernel, nx, ny),
             out_shape=(
                 pltpu.VMEM(flat, jnp.float32),
-                pltpu.VMEM((depth // nx, width * nx, length), jnp.float32),
+                pltpu.VMEM(deep, jnp.float32),
             ),
             in_specs=[hbm] * 8,
             out_specs=(vmem, vmem),
@@ -464,8 +467,7 @@
                 pltpu.VMEM((width, length), jnp.int32),
                 pltpu.VMEM((width, length), jnp.int32),
                 pltpu.VMEM((width, length), jnp.int32),
-                pltpu.SemaphoreType.DMA((parts,)),
-                pltpu.SemaphoreType.DMA((7,)),
+                pltpu.SemaphoreType.DMA((8,)),
                 pltpu.SemaphoreType.DMA((2, parts, 2)),
                 pltpu.SemaphoreType.DMA((2, parts, 2)),
                 pltpu.SemaphoreType.DMA((2, parts, 2) if ny > 1 else (1, 1, 1)),
@@ -478,6 +480,17 @@
                 collective_id=0, has_side_effects=True, vmem_limit_bytes=60000000
             ),
         )(pressure, prior, courant, wavelet, delay, sdepth, rdepth, receiver)
+        return pl.pallas_call(
+            store,
+            out_shape=(
+                jax.ShapeDtypeStruct(flat, jnp.float32),
+                jax.ShapeDtypeStruct(deep, jnp.float32),
+            ),
+            in_specs=[vmem] * 2,
+            out_specs=(hbm, hbm),
+            scratch_shapes=[pltpu.SemaphoreType.DMA((2,))],
+            compiler_params=pltpu.CompilerParams(vmem_limit_bytes=4 << 20),
+        )(*(pltpu.with_memory_space_constraint(part, pltpu.VMEM) for part in held))
 
     in_specs = (
         P(None, ("shots", "gx"), "gy"),

time: 63.4 us -> 62.8 us (level)
  local copies, waits for them, and re-layouts: 1.59 us -> 0 us
  Pallas kernels: 61 us -> 62 us
    unnamed x2 -> x0, local copies, waits for them, and re-layouts: 1.59 us -> none
    pallas_call x0 -> x1, Pallas kernels: none -> 0.99 us  [shards(): pl.pallas_call(store, out_shape=(jax.ShapeDtypeStruct(flat, jnp.float32),...]
where the time goes in v3:
time: 62.8 us; the launch traced here: 62.6 us
  Pallas kernels  62 us (99%)
  between operations  0.64 us (1%)
    pallas_call x1, Pallas kernels, shards(): pl.pallas_call(functools.partial(kernel, nx, ny), out_shape=(pltpu.VMEM(f...  61 us

profile of v3, /device:TPU:15, one launch (start us, length us, event | category | flops | bytes accessed | tf_op | source)
XLA Modules:
  0.0 62.6 jit_solution(1419274994287340821)
XLA Ops:
  0.6 61.0 %shard_map.95 = (f32[128,8,128]{2,1,0:T(8,128)S(1)}, f32[4,256,128]{2,1,0:T(8,128)S(1)}) custom-call(f32[128,8,128]{2,1,0:T(8,128)} %pressure.1, f32[128,8,128]{2,1,0:T(8,128)} %prior.1, bf16[128,8,128]{2,1,0:T(8,128)(2,1)} %courant.1, f32[16]{0:T(128)} %wavelet.1, s32[8,128]{1,0:T(8,128)} %delay.1, s32[8,128]{1,0:T(8,128)} %sdepth.1, s32[8,128]{1,0:T(8,128)} %rdepth.1, ...), custom_call_target="tpu_custom_call" | custom-call | tf_op jit(solution)/shard_map/pallas_call | solution.py:449
  61.7 1.0 %shard_map.96 = (f32[128,8,128]{2,1,0:T(8,128)}, f32[4,256,128]{2,1,0:T(8,128)}) custom-call(f32[128,8,128]{2,1,0:T(8,128)S(1)} %get-tuple-element.4.final_v, f32[4,256,128]{2,1,0:T(8,128)S(1)} %get-tuple-element.5.image_v), custom_call_target="tpu_custom_call" | custom-call | tf_op jit(solution)/shard_map/pallas_call | solution.py:483

commit v4 on v3

--- a/solution.py
+++ b/solution.py
@@ -36,6 +36,7 @@
     side,
     courant_v,
     receiver_v,
+    partial,
     amp,
     product,
     slab,
@@ -109,8 +110,8 @@
             if opening
             else field.at[t + 1, span(c), pl.ds(REACH + source, REACH), :],
             dst_ref=field.at[t + 1, span(c), pl.ds(target, REACH), :],
-            send_sem=send_sem.at[t % 2, c, way],
-            recv_sem=recv_sem.at[t % 2, c, way],
+            send_sem=send_sem.at[t % 2],
+            recv_sem=recv_sem.at[t % 2, c],
             device_id={"gx": lax.rem(me + (1 if way == 0 else nx - 1), nx)},
             device_id_type=pl.DeviceIdType.MESH,
         )
@@ -129,31 +130,66 @@
             device_id_type=pl.DeviceIdType.MESH,
         )
 
-    def each_face(t, c, act, sending, opening=False):
+    def send(t, c, opening=False):
         if nx > 1:
             for way in (0, 1):
-                there = me < nx - 1 if (way == 0) == sending else me > 0
-
-                @pl.when(there)
+
+                @pl.when(me < nx - 1 if way == 0 else me > 0)
                 def _():
-                    act(face(t, c, way, opening))
+                    face(t, c, way, opening).start()
 
         if ny > 1:
             for way in (0, 1):
-                there = mine < ny - 1 if (way == 0) == sending else mine > 0
-
-                @pl.when(there)
+
+                @pl.when(mine < ny - 1 if way == 0 else mine > 0)
                 def _():
-                    act(flank(t, c, way, opening))
-
-    def send(t, c, opening=False):
-        each_face(t, c, lambda copy: copy.start(), True, opening)
-
-    def sent(t, c):
-        each_face(t, c, lambda copy: copy.wait_send(), True)
+                    flank(t, c, way, opening).start()
+
+    def faces(t, begin, rows, ways, c):
+        both = field.at[t + 1, pl.ds(REACH + begin, rows), pl.ds(0, ways * REACH), :]
+        return pltpu.make_async_remote_copy(
+            src_ref=both,
+            dst_ref=both,
+            send_sem=send_sem.at[t % 2],
+            recv_sem=recv_sem.at[t % 2, c],
+            device_id={"gx": lax.rem(me + 1, nx)},
+            device_id_type=pl.DeviceIdType.MESH,
+        )
+
+    edge = jnp.logical_or(me == 0, me == nx - 1)
+
+    def each_count(act):
+        if nx > 1:
+
+            @pl.when(edge)
+            def _():
+                act(1)
+
+        if nx > 2:
+
+            @pl.when(jnp.logical_not(edge))
+            def _():
+                act(2)
+
+    def sent(t):
+        each_count(lambda ways: faces(t, 0, depth, ways, 0).wait_send())
+        if ny > 1:
+            for way in (0, 1):
+
+                @pl.when(mine < ny - 1 if way == 0 else mine > 0)
+                def _():
+                    for c in range(len(chunks)):
+                        flank(t, c, way, False).wait_send()
 
     def arrived(t, c):
-        each_face(t, c, lambda copy: copy.wait_recv(), False)
+        begin, rows = chunks[c]
+        each_count(lambda ways: faces(t, begin, rows, ways, c).wait_recv())
+        if ny > 1:
+            for way in (0, 1):
+
+                @pl.when(mine > 0 if way == 0 else mine < ny - 1)
+                def _():
+                    flank(t, c, way, False).wait_recv()
 
     beside = (me > 0).astype(jnp.int32) + (me < nx - 1).astype(jnp.int32)
     if nx > 1 or ny > 1:
@@ -242,33 +278,48 @@
         )
         return (both[:, :length] + both[:, length:]).reshape(GROUP, width, length)
 
-    def advance(t, z):
+    def prepare(t, z):
         at = t + 1
         v = field[at, pl.ds(REACH + z, GROUP), own, :]
         old = field[t, pl.ds(REACH + z, GROUP), own, :]
         total = (3.0 * CENTER) * v if ny > 1 else along(v)
         for k in range(1, REACH + 1):
-            near = (
+            total = total + COEFS[k - 1] * (
                 field[at, pl.ds(REACH + z + k, GROUP), own, :]
                 + field[at, pl.ds(REACH + z - k, GROUP), own, :]
             )
-            near = near + (
+        strength = courant_v[pl.ds(z, GROUP), :, :].astype(jnp.float32)
+        levels = lax.broadcasted_iota(jnp.int32, (GROUP, width, length), 0) + z
+        shot = jnp.where(levels == origin[None], amp[t][None], 0.0)
+        partial[pl.ds(z, GROUP), :, :] = 2.0 * v - old + strength * total + shot
+
+    def complete(t, z):
+        at = t + 1
+        total = None
+        for k in range(1, REACH + 1):
+            near = (
                 field[at, pl.ds(REACH + z, GROUP), pl.ds(REACH + k, width), :]
                 + field[at, pl.ds(REACH + z, GROUP), pl.ds(REACH - k, width), :]
             )
-            total = total + COEFS[k - 1] * near
             if ny > 1:
+                v = field[at, pl.ds(REACH + z, GROUP), own, :]
                 up = pltpu.roll(v, length - k, 2)
                 down = pltpu.roll(v, k, 2)
                 low = pltpu.roll(side[t, 0, pl.ds(z, GROUP), :, :], k, 2)
                 high = pltpu.roll(side[t, 1, pl.ds(z, GROUP), :, :], length - k, 2)
                 up = jnp.where((lanes < length - k)[None], up, high)
                 down = jnp.where((lanes >= k)[None], down, low)
-                total = total + COEFS[k - 1] * (up + down)
+                near = near + (up + down)
+            total = COEFS[k - 1] * near if k == 1 else total + COEFS[k - 1] * near
         strength = courant_v[pl.ds(z, GROUP), :, :].astype(jnp.float32)
-        levels = lax.broadcasted_iota(jnp.int32, (GROUP, width, length), 0) + z
-        shot = jnp.where(levels == origin[None], amp[t][None], 0.0)
-        return 2.0 * v - old + strength * total + shot
+        return partial[pl.ds(z, GROUP), :, :] + strength * total
+
+    def prepared(t, begin, rows):
+        def group(g, inner):
+            prepare(t, begin + g * GROUP)
+            return inner
+
+        lax.fori_loop(0, rows // GROUP, group, 0, unroll=True)
 
     reach = []
     while (reach[-1] * 2 if reach else 1) < nx:
@@ -308,16 +359,17 @@
                 def _():
                     meet(number)
 
+        @pl.when(t > 0)
+        def _():
+            sent(t - 1)
+
         for c, (begin, rows) in enumerate(chunks):
+            prepared(t, begin, rows)
             arrived(t, c)
-
-            @pl.when(t > 0)
-            def _():
-                sent(t - 1, c)
 
             def group(g, inner):
                 z = begin + g * GROUP
-                field[t + 2, pl.ds(REACH + z, GROUP), own, :] = advance(t, z)
+                field[t + 2, pl.ds(REACH + z, GROUP), own, :] = complete(t, z)
                 return inner
 
             lax.fori_loop(0, rows // GROUP, group, 0, unroll=True)
@@ -375,11 +427,12 @@
     last = STEPS - 1
     ready, gone = set(), set()
     for c, (begin, rows) in enumerate(chunks):
+        prepared(last, begin, rows)
         arrived(last, c)
 
         def group(g, inner):
             z = begin + g * GROUP
-            new = advance(last, z)
+            new = complete(last, z)
             final[pl.ds(z, GROUP), :, :] = new
             levels = lax.broadcasted_iota(jnp.int32, (GROUP, width, length), 0) + z
             masked = jnp.where(levels >= ground[None], receiver_v[pl.ds(z, GROUP), :, :], 0.0)
@@ -409,8 +462,7 @@
             low = high
 
     for t in range(max(STEPS - 2, 0), STEPS):
-        for c in range(len(chunks)):
-            sent(t, c)
+        sent(t)
     if nx > 1:
         others = pltpu.make_async_remote_copy(
             src_ref=slab.at[pl.ds(0, (nx - 1) * slab_depth), :, :],
@@ -459,6 +511,7 @@
                 pltpu.VMEM(sides, jnp.float32),
                 pltpu.VMEM(flat, jnp.bfloat16),
                 pltpu.VMEM(flat, jnp.float32),
+                pltpu.VMEM(flat, jnp.float32),
                 pltpu.VMEM((STEPS, width, length), jnp.float32),
                 pltpu.VMEM((depth + 2, width, length), jnp.float32),
                 pltpu.VMEM(flat, jnp.float32),
@@ -468,8 +521,8 @@
                 pltpu.VMEM((width, length), jnp.int32),
                 pltpu.VMEM((width, length), jnp.int32),
                 pltpu.SemaphoreType.DMA((8,)),
-                pltpu.SemaphoreType.DMA((2, parts, 2)),
-                pltpu.SemaphoreType.DMA((2, parts, 2)),
+                pltpu.SemaphoreType.DMA((2,)),
+                pltpu.SemaphoreType.DMA((2, parts)),
                 pltpu.SemaphoreType.DMA((2, parts, 2) if ny > 1 else (1, 1, 1)),
                 pltpu.SemaphoreType.DMA((2, parts, 2) if ny > 1 else (1, 1, 1)),
                 pltpu.SemaphoreType.DMA,

time: 62.8 us -> 62.2 us (level)
  no operation moved by 1% of the time
where the time goes in v4:
time: 62.2 us; the launch traced here: 62.1 us
  Pallas kernels  61.4 us (99%)
  between operations  0.64 us (1%)
    pallas_call x1, Pallas kernels, shards(): pl.pallas_call(functools.partial(kernel, nx, ny), out_shape=(pltpu.VMEM(f...  60.4 us

profile of v4, /device:TPU:15, one launch (start us, length us, event | category | flops | bytes accessed | tf_op | source)
XLA Modules:
  0.0 62.1 jit_solution(16724542140556351237)
XLA Ops:
  0.6 60.4 %shard_map.95 = (f32[128,8,128]{2,1,0:T(8,128)S(1)}, f32[4,256,128]{2,1,0:T(8,128)S(1)}) custom-call(f32[128,8,128]{2,1,0:T(8,128)} %pressure.1, f32[128,8,128]{2,1,0:T(8,128)} %prior.1, bf16[128,8,128]{2,1,0:T(8,128)(2,1)} %courant.1, f32[16]{0:T(128)} %wavelet.1, s32[8,128]{1,0:T(8,128)} %delay.1, s32[8,128]{1,0:T(8,128)} %sdepth.1, s32[8,128]{1,0:T(8,128)} %rdepth.1, ...), custom_call_target="tpu_custom_call" | custom-call | tf_op jit(solution)/shard_map/pallas_call | solution.py:501
  61.1 1.0 %shard_map.96 = (f32[128,8,128]{2,1,0:T(8,128)}, f32[4,256,128]{2,1,0:T(8,128)}) custom-call(f32[128,8,128]{2,1,0:T(8,128)S(1)} %get-tuple-element.4.final_v, f32[4,256,128]{2,1,0:T(8,128)S(1)} %get-tuple-element.5.image_v), custom_call_target="tpu_custom_call" | custom-call | tf_op jit(solution)/shard_map/pallas_call | solution.py:536

commit v5 on v4

--- a/solution.py
+++ b/solution.py
@@ -16,7 +16,7 @@
 
 def chunks_of(depth):
     quarter = depth // 4
-    return tuple((quarter * c, quarter) for c in (0, 3, 1, 2))
+    return tuple((quarter * c, quarter) for c in (0, 2, 1, 3))
 
 
 def kernel(
@@ -42,9 +42,7 @@
     slab,
     weights,
     wave_v,
-    delay_v,
-    sdepth_v,
-    rdepth_v,
+    small_v,
     local_sem,
     send_sem,
     recv_sem,
@@ -91,11 +89,11 @@
         pltpu.make_async_copy(prior, field.at[0, pl.ds(REACH, depth), own, :], local_sem.at[0]),
         pltpu.make_async_copy(courant, courant_v, local_sem.at[1]),
         pltpu.make_async_copy(wavelet, wave_v, local_sem.at[2]),
-        pltpu.make_async_copy(delay, delay_v, local_sem.at[3]),
-        pltpu.make_async_copy(sdepth, sdepth_v, local_sem.at[4]),
-        pltpu.make_async_copy(rdepth, rdepth_v, local_sem.at[5]),
-        pltpu.make_async_copy(receiver, receiver_v, local_sem.at[6]),
-        pltpu.make_async_copy(pressure, field.at[1, pl.ds(REACH, depth), own, :], local_sem.at[7]),
+        pltpu.make_async_copy(delay, small_v.at[0], local_sem.at[3]),
+        pltpu.make_async_copy(sdepth, small_v.at[1], local_sem.at[3]),
+        pltpu.make_async_copy(rdepth, small_v.at[2], local_sem.at[3]),
+        pltpu.make_async_copy(receiver, receiver_v, local_sem.at[4]),
+        pltpu.make_async_copy(pressure, field.at[1, pl.ds(REACH, depth), own, :], local_sem.at[0]),
     ]
     def span(c):
         z, rows = chunks[c]
@@ -257,9 +255,12 @@
         axis=0,
     )
 
-    for copy in local[:6] + local[7:]:
-        copy.wait()
-    late = delay_v[...]
+    fields = field.at[pl.ds(0, 2), pl.ds(REACH, depth), own, :]
+    pltpu.make_async_copy(fields, fields, local_sem.at[0]).wait()
+    local[1].wait()
+    local[2].wait()
+    pltpu.make_async_copy(small_v, small_v, local_sem.at[3]).wait()
+    late = small_v[0]
     for t in range(STEPS):
         total = jnp.zeros((width, length), jnp.float32)
         for pick in range(wavelet.shape[0]):
@@ -267,7 +268,7 @@
         amp[t] = total
 
     lanes = lax.broadcasted_iota(jnp.int32, (width, length), 1)
-    origin = sdepth_v[...]
+    origin = small_v[1]
 
     def along(v):
         tall = v.reshape(GROUP * width, length)
@@ -423,7 +424,7 @@
         lax.fori_loop(0, count, one, 0)
 
     local[6].wait()
-    ground = rdepth_v[...]
+    ground = small_v[2]
     last = STEPS - 1
     ready, gone = set(), set()
     for c, (begin, rows) in enumerate(chunks):
@@ -517,10 +518,8 @@
                 pltpu.VMEM(flat, jnp.float32),
                 pltpu.VMEM((2 * length, 2 * length), jnp.bfloat16),
                 pltpu.SMEM(wavelet.shape, jnp.float32),
-                pltpu.VMEM((width, length), jnp.int32),
-                pltpu.VMEM((width, length), jnp.int32),
-                pltpu.VMEM((width, length), jnp.int32),
-                pltpu.SemaphoreType.DMA((8,)),
+                pltpu.VMEM((3, width, length), jnp.int32),
+                pltpu.SemaphoreType.DMA((5,)),
                 pltpu.SemaphoreType.DMA((2,)),
                 pltpu.SemaphoreType.DMA((2, parts)),
                 pltpu.SemaphoreType.DMA((2, parts, 2) if ny > 1 else (1, 1, 1)),

time: 62.2 us -> 62.1 us (level); the launches traced: 62.1 us -> 60.9 us
  Pallas kernels: 61.4 us -> 60.2 us
    pallas_call x1, Pallas kernels: 60.4 us -> 59.2 us  [shards(): pl.pallas_call(functools.partial(kernel, nx, ny), out_shape=(pltpu.VMEM(f...]
where the time goes in v5:
time: 62.1 us; the launch traced here: 60.9 us
  Pallas kernels  60.2 us (97%)
  between operations  0.64 us (1%)
    pallas_call x1, Pallas kernels, shards(): pl.pallas_call(functools.partial(kernel, nx, ny), out_shape=(pltpu.VMEM(f...  59.2 us

profile of v5, /device:TPU:15, one launch (start us, length us, event | category | flops | bytes accessed | tf_op | source)
XLA Modules:
  0.0 60.9 jit_solution(15284335046126225872)
XLA Ops:
  0.6 59.2 %shard_map.95 = (f32[128,8,128]{2,1,0:T(8,128)S(1)}, f32[4,256,128]{2,1,0:T(8,128)S(1)}) custom-call(f32[128,8,128]{2,1,0:T(8,128)} %pressure.1, f32[128,8,128]{2,1,0:T(8,128)} %prior.1, bf16[128,8,128]{2,1,0:T(8,128)(2,1)} %courant.1, f32[16]{0:T(128)} %wavelet.1, s32[8,128]{1,0:T(8,128)} %delay.1, s32[8,128]{1,0:T(8,128)} %sdepth.1, s32[8,128]{1,0:T(8,128)} %rdepth.1, ...), custom_call_target="tpu_custom_call" | custom-call | tf_op jit(solution)/shard_map/pallas_call | solution.py:502
  59.9 1.0 %shard_map.96 = (f32[128,8,128]{2,1,0:T(8,128)}, f32[4,256,128]{2,1,0:T(8,128)}) custom-call(f32[128,8,128]{2,1,0:T(8,128)S(1)} %get-tuple-element.4.final_v, f32[4,256,128]{2,1,0:T(8,128)S(1)} %get-tuple-element.5.image_v), custom_call_target="tpu_custom_call" | custom-call | tf_op jit(solution)/shard_map/pallas_call | solution.py:535
